TPU v7x, 32 devices: a whole 2x2x4 slice. The times are simulated.
32 devices in a mesh: aux: 8 (over y, x, core), pair: 4 (over z).
Axes of the slice: x: 2, y: 2, z: 4, core: 2. Of those that a mesh axis runs over, the one named last changes fastest.
Arguments:
- integrals: bfloat16 [3072, 32768], P('aux', 'pair'), may hold values from -0.15625 to 0.15625
- densities: bfloat16 [16, 32768], P(None, 'pair'), may hold values from -2.390625 to 2.390625
- screen: int32 [24, 256], P('aux', 'pair'), may hold values 0 or 1
- factor: float32 [3072, 3072], P('aux', 'pair'), may hold values from -0.109375 to 0.109375
- diag_inv: float32 [3072, 768], P('aux'), may hold values from -2 to 2, as said below
Outputs:
- coulomb: float32 [16, 32768], P(None, ('pair', 'aux'))
Inputs may be any that keep to these rules, and one draw needn't show every extreme that they name: `diag_inv`: each block of 768 rows is an upper triangular matrix with a positive diagonal.
All inputs are finite; a program needn't handle non-finite values. No bound on the sum of `screen` on one device may be relied on, other than what follows from the above.
Results may differ from a plain program's by a relative error of at most 0.0041.
Values may be sent and summed in bfloat16 or wider, within the bound.
A program may use at most 128 MiB of HBM per device.

v0:
```python
import jax
import jax.numpy as jnp
from jax import lax
from jax.sharding import PartitionSpec as P

TILE = 128
SOLVE_BLOCKS = 4


def shards(integrals, densities, screen, factor, diag_inv):
    height = integrals.shape[0]
    breadth = factor.shape[1]
    block_size = diag_inv.shape[1]
    rows_aux = lax.axis_size("aux")
    total = height * rows_aux
    members = rows_aux // SOLVE_BLOCKS
    my_row = lax.axis_index("aux")
    my_column = lax.axis_index("pair")
    my_block = my_row // members
    count = densities.shape[0]
    highest = lax.Precision.HIGHEST
    expanded = jnp.repeat(jnp.repeat(screen, TILE, axis=0), TILE, axis=1).astype(jnp.bfloat16)
    masked = integrals * expanded
    partial_fit = lax.dot_general(
        densities, masked, (((1,), (1,)), ((), ())), preferred_element_type=jnp.float32
    )
    column_block = (my_column * breadth + jnp.arange(breadth, dtype=jnp.int32)) // block_size
    factor_low = jnp.where((column_block < my_block)[None, :], factor, 0.0)

    def apply_inverse(values):
        return jnp.dot(values, diag_inv, precision=highest, preferred_element_type=jnp.float32)

    def own_columns(whole):
        return lax.dynamic_slice_in_dim(whole, my_column * breadth, breadth, 1)

    def times_factor(known):
        return lax.dot_general(
            known,
            factor_low,
            (((1,), (1,)), ((), ())),
            precision=highest,
            preferred_element_type=jnp.float32,
        )

    zero_block = jnp.zeros((count, block_size), jnp.float32)
    solved = jnp.zeros((count, total), jnp.float32)
    for k in range(SOLVE_BLOCKS):

        def on_group(current):
            return apply_inverse(partial_fit - times_factor(own_columns(current)))

        def off_group(current):
            return zero_block

        summand = lax.cond(my_block == k, on_group, off_group, solved)
        arrived = lax.psum(summand, ("aux", "pair"))
        solved = lax.dynamic_update_slice_in_dim(solved, arrived, k * block_size, 1)
    own_coef = jnp.zeros((count, height), jnp.float32)
    contrib = jnp.zeros((count, total), jnp.float32)
    for target in reversed(range(SOLVE_BLOCKS)):
        if target < SOLVE_BLOCKS - 1:
            portion = contrib[:, target * block_size : (target + 1) * block_size]
            behind = lax.psum(portion, ("aux", "pair"))
            settled = solved[:, target * block_size : (target + 1) * block_size] - behind
        else:
            settled = solved[:, target * block_size : (target + 1) * block_size]

        def on_group(state):
            coef = lax.dot_general(
                settled,
                diag_inv,
                (((1,), (1,)), ((), ())),
                precision=highest,
                preferred_element_type=jnp.float32,
            )
            if target > 0:
                spread_out = jnp.dot(
                    coef, factor_low, precision=highest, preferred_element_type=jnp.float32
                )
                fresh = lax.dynamic_update_slice_in_dim(
                    jnp.zeros((count, total), jnp.float32), spread_out, my_column * breadth, 1
                )
            else:
                fresh = state[1]
            return (coef, fresh)

        def keep_state(state):
            return state

        own_coef, contrib = lax.cond(my_block == target, on_group, keep_state, (own_coef, contrib))
    rounded = own_coef.astype(jnp.bfloat16)
    summand = jnp.dot(rounded, masked, preferred_element_type=jnp.float32)
    result = lax.psum_scatter(summand, "aux", scatter_dimension=1, tiled=True)
    return result


def solution(mesh):
    in_specs = (
        P("aux", "pair"),
        P(None, "pair"),
        P("aux", "pair"),
        P("aux", "pair"),
        P("aux", None),
    )
    out_specs = P(None, ("pair", "aux"))
    return jax.shard_map(shards, mesh=mesh, in_specs=in_specs, out_specs=out_specs, check_vma=False)
```

profile of v0, /device:TPU:0, one launch (start us, length us, event | category | flops | bytes accessed | tf_op | source)
XLA Modules:
  0.0 370.9 jit_solution(1663735948647780986)
XLA Ops:
  6.5 0.0 copy-start
  6.5 0.0 reduce-scatter.2.cloned.1.call-start
  6.6 0.7 convert_element_type.40
  7.3 1.3 broadcast_select_fusion
  8.7 0.0 copy-start.3
  8.7 3.8 %broadcast_in_dim.25 = bf16[384,64,128]{2,1,0:T(8,128)(2,1)S(1)} broadcast(bf16[384,64]{1,0:T(8,128)(2,1)S(1)} %bitcast.36), dimensions={0,1} | broadcast | bytes 6340608 | tf_op jit(solution)/shard_map/broadcast_in_dim | solution.py:22
  12.5 0.0 copy-start.2
  12.5 0.0 copy-done
  12.5 0.0 copy-done.3
  12.5 0.0 copy-start.1
  12.6 4.0 %fusion.18 = f32[16,384]{1,0:T(8,128)S(1)} fusion(bf16[16,8192]{1,0:T(8,128)(2,1)S(1)} %copy-done, bf16[384,8192]{1,0:T(8,128)(2,1)S(1)} %copy-done.3, bf16[48,8,64,128]{3,2,1,0:T(8,128)(2,1)S(1)} %bitcast.34), kind=kOutput, calls=%fused_computation.26 | convolution fusion | flops 103809024 | bytes 12869632 | tf_op jit(solution)/shard_map/dot_general | solution.py:24
  16.5 0.0 copy-done.2
  16.5 0.0 copy-done.1
  16.5 1.8 conditional.8
  16.6 1.1 convolution_subtract_fusion
  17.6 0.7 fusion.22
  18.3 41.4 %psum.49 = f32[16,768]{1,0:T(8,128)S(1)} all-reduce(f32[16,768]{1,0:T(8,128)S(1)} %get-tuple-element.168), channel_id=1, replica_groups=mesh['aux'=8,'pair'=4] {'aux','pair'}, use_global_device_ids=true, to_apply=%region_2.3 | all-reduce | flops 12288 | bytes 98304 | tf_op jit(solution)/shard_map/psum | solution.py:56
  59.8 41.6 %psum.50 = f32[16,768]{1,0:T(8,128)S(1)} all-reduce(f32[16,768]{1,0:T(8,128)S(1)} %get-tuple-element.169), channel_id=1, replica_groups=mesh['aux'=8,'pair'=4] {'aux','pair'}, use_global_device_ids=true, to_apply=%region_5.6 | all-reduce | flops 12288 | bytes 98304 | tf_op jit(solution)/shard_map/psum | solution.py:56
  101.5 40.8 %psum.51 = f32[16,768]{1,0:T(8,128)S(1)} all-reduce(f32[16,768]{1,0:T(8,128)S(1)} %get-tuple-element.170), channel_id=1, replica_groups=mesh['aux'=8,'pair'=4] {'aux','pair'}, use_global_device_ids=true, to_apply=%region_8.9 | all-reduce | flops 12288 | bytes 98304 | tf_op jit(solution)/shard_map/psum | solution.py:56
  142.3 0.2 conditional.11
  142.5 43.4 %psum.52 = f32[16,768]{1,0:T(8,128)S(1)} all-reduce(f32[16,768]{1,0:T(8,128)S(1)} %get-tuple-element.171), channel_id=1, replica_groups=mesh['aux'=8,'pair'=4] {'aux','pair'}, use_global_device_ids=true, to_apply=%region_11.12 | all-reduce | flops 12288 | bytes 98304 | tf_op jit(solution)/shard_map/psum | solution.py:56
  185.9 1.3 conditional.12
  185.9 0.6 broadcast_in_dim.17
  186.5 0.7 broadcast.57
  187.2 0.8 slice.19
  188.0 42.1 %psum.53 = f32[16,768]{1,0:T(8,128)S(1)} all-reduce(f32[16,768]{1,0:T(8,128)S(1)} %slice.19), channel_id=1, replica_groups=mesh['aux'=8,'pair'=4] {'aux','pair'}, use_global_device_ids=true, to_apply=%region_14.15 | all-reduce | flops 12288 | bytes 98304 | tf_op jit(solution)/shard_map/psum | solution.py:63
  230.1 0.8 slice.20
  230.9 44.2 %psum.54 = f32[16,768]{1,0:T(8,128)S(1)} all-reduce(f32[16,768]{1,0:T(8,128)S(1)} %slice.20), channel_id=1, replica_groups=mesh['aux'=8,'pair'=4] {'aux','pair'}, use_global_device_ids=true, to_apply=%region_17.18 | all-reduce | flops 12288 | bytes 98304 | tf_op jit(solution)/shard_map/psum | solution.py:63
  275.1 0.8 slice.21
  276.0 43.3 %psum.55 = f32[16,768]{1,0:T(8,128)S(1)} all-reduce(f32[16,768]{1,0:T(8,128)S(1)} %slice.21), channel_id=1, replica_groups=mesh['aux'=8,'pair'=4] {'aux','pair'}, use_global_device_ids=true, to_apply=%region_20.21 | all-reduce | flops 12288 | bytes 98304 | tf_op jit(solution)/shard_map/psum | solution.py:63
  319.3 1.7 conditional.15
  319.3 1.7 fusion.13
  321.0 9.1 %fusion.16 = f32[16,8192]{1,0:T(8,128)} fusion(bf16[384,8192]{1,0:T(8,128)(2,1)} %param.21, bf16[48,8,64,128]{3,2,1,0:T(8,128)(2,1)} %bitcast.35, f32[16,384]{1,0:T(8,128)} %get-tuple-element.174), kind=kOutput, calls=%fused_computation.24 | convolution fusion | flops 103815168 | bytes 13131776 | tf_op jit(solution)/shard_map/dot_general | solution.py:92
  330.1 0.0 reduce-scatter.2.cloned.1.call-update
  330.1 33.9 %reduce-scatter.2.cloned.1.call-done = f32[16,1024]{1,0:T(8,128)} async-done(((f32[16,8192]{1,0:T(8,128)}), f32[16,1024]{1,0:T(8,128)}) %reduce-scatter.2.cloned.1.call-update) | async-done | bytes 65552 | tf_op jit(solution)/shard_map/reduce_scatter | solution.py:93
  (12 shorter events, 0.1 us)
Async XLA Ops:
  6.5 6.0 %copy-start = (bf16[16,8192]{1,0:T(8,128)(2,1)S(1)}, bf16[16,8192]{1,0:T(8,128)(2,1)}, u32[]{:S(2)}) copy-start(bf16[16,8192]{1,0:T(8,128)(2,1)} %param.22) | copy-start | bytes 786436
  6.5 357.5 %reduce-scatter.2.cloned.1.call-start = ((), (), s32[]{:S(2)}) async-start(), calls=%async_computation.1 | async-start | bytes 589824 | tf_op jit(solution)/shard_map/reduce_scatter | solution.py:93
  8.7 3.9 %copy-start.3 = (bf16[384,8192]{1,0:T(8,128)(2,1)S(1)}, bf16[384,8192]{1,0:T(8,128)(2,1)}, u32[]{:S(2)}) copy-start(bf16[384,8192]{1,0:T(8,128)(2,1)} %param.21) | copy-start | bytes 18874372
  12.5 4.0 %copy-start.2 = (bf16[384,64,128]{2,1,0:T(8,128)(2,1)}, bf16[384,64,128]{2,1,0:T(8,128)(2,1)S(1)}, u32[]{:S(2)}) copy-start(bf16[384,64,128]{2,1,0:T(8,128)(2,1)S(1)} %broadcast_in_dim.25) | copy-start | bytes 18874372
  12.5 4.0 %copy-start.1 = (f32[384,768]{1,0:T(8,128)S(1)}, f32[384,768]{1,0:T(8,128)}, u32[]{:S(2)}) copy-start(f32[384,768]{1,0:T(8,128)} %param.25) | copy-start | bytes 3538948
Sparse Core Ops, SparseCore 0:
  330.2 33.7 reduce-scatter.1
where the time goes:
time: 372 us; the launch traced here: 371 us
  blocking collectives  297 us (80%)
  waiting for transfers between devices  34 us (9%)
  matrix products  16.6 us (4%)
  between operations  13.6 us (4%)
  local copies, waits for them, and re-layouts  7.62 us (2%)
    psum x4, blocking collectives, shards(): arrived = lax.psum(summand, ('aux', 'pair'))  167 us
    psum x3, blocking collectives, shards(): behind = lax.psum(portion, ('aux', 'pair'))  130 us
    reduce_scatter x1, waiting for transfers between devices, shards(): result = lax.psum_scatter(summand, 'aux', scatter_dimension=1, tiled=True)  33.9 us
    dot_general x1, matrix products, shards(): summand = jnp.dot(rounded, masked, preferred_element_type=jnp.float32)  9.1 us
  transfers between devices with their start and end apart: 1, of which 1 were waited for; matrix products, arithmetic and copies ran while one was open for 0% of the time, Pallas kernels for 0%

commit v1 on v0

--- a/solution.py
+++ b/solution.py
@@ -60,7 +60,8 @@
     for target in reversed(range(SOLVE_BLOCKS)):
         if target < SOLVE_BLOCKS - 1:
             portion = contrib[:, target * block_size : (target + 1) * block_size]
-            behind = lax.psum(portion, ("aux", "pair"))
+            perform_the_run = lambda x0: jnp.sum(lax.all_gather(x0, ("aux", "pair")), axis=0)
+            behind = perform_the_run(portion)
             settled = solved[:, target * block_size : (target + 1) * block_size] - behind
         else:
             settled = solved[:, target * block_size : (target + 1) * block_size]

time: 372 us -> 421 us (1.13)
  waiting for transfers between devices: 34 us -> 210 us
  blocking collectives: 297 us -> 167 us
    all_gather x0 -> x3, waiting for transfers between devices: none -> 177 us  [shards(): lax.all_gather(x0, ('aux', 'pair'))]
    psum x3 -> x0, blocking collectives: 130 us -> none  [shards(): behind = lax.psum(portion, ('aux', 'pair'))]
  transfers between devices with their start and end apart: 1 -> 4, of which waited for: 1 -> 4; matrix products, arithmetic and copies ran while one was open for 0% -> 0% of each run, Pallas kernels for 0% -> 0%
where the time goes in v1:
time: 421 us; the launch traced here: 420 us
  waiting for transfers between devices  210 us (50%)
  blocking collectives  167 us (40%)
  matrix products  16.6 us (4%)
  between operations  13.3 us (3%)
  local copies, waits for them, and re-layouts  9.47 us (2%)
    all_gather x3, waiting for transfers between devices, shards(): lax.all_gather(x0, ('aux', 'pair'))  177 us
    psum x4, blocking collectives, shards(): arrived = lax.psum(summand, ('aux', 'pair'))  167 us
    reduce_scatter x1, waiting for transfers between devices, shards(): result = lax.psum_scatter(summand, 'aux', scatter_dimension=1, tiled=True)  32.3 us
    dot_general x1, matrix products, shards(): summand = jnp.dot(rounded, masked, preferred_element_type=jnp.float32)  9.12 us
  transfers between devices with their start and end apart: 4, of which 4 were waited for; matrix products, arithmetic and copies ran while one was open for 0% of the time, Pallas kernels for 0%

profile of v1, /device:TPU:0, one launch (start us, length us, event | category | flops | bytes accessed | tf_op | source)
XLA Modules:
  0.0 420.2 jit_solution(17415658657768113657)
XLA Ops:
  6.5 0.0 copy-start
  6.5 0.0 all-gather.7.cloned.1.call-start
  6.6 0.7 convert_element_type.40
  7.3 1.3 broadcast_select_fusion
  8.7 0.0 copy-start.3
  8.7 3.8 broadcast_in_dim.25
  12.5 0.0 copy-start.2
  12.5 0.0 copy-done
  12.5 0.0 copy-done.3
  12.5 0.0 copy-start.1
  12.6 4.0 fusion.18
  16.5 0.0 copy-done.2
  16.5 0.0 copy-done.1
  16.5 1.8 conditional.8
  16.6 1.1 convolution_subtract_fusion
  17.6 0.7 fusion.22
  18.3 41.4 %psum.28 = f32[16,768]{1,0:T(8,128)S(1)} all-reduce(f32[16,768]{1,0:T(8,128)S(1)} %get-tuple-element.174), channel_id=1, replica_groups=mesh['aux'=8,'pair'=4] {'aux','pair'}, use_global_device_ids=true, to_apply=%region_2.3 | all-reduce | flops 12288 | bytes 98304 | tf_op jit(solution)/shard_map/psum | solution.py:56
  59.8 41.6 %psum.29 = f32[16,768]{1,0:T(8,128)S(1)} all-reduce(f32[16,768]{1,0:T(8,128)S(1)} %get-tuple-element.175), channel_id=1, replica_groups=mesh['aux'=8,'pair'=4] {'aux','pair'}, use_global_device_ids=true, to_apply=%region_5.6 | all-reduce | flops 12288 | bytes 98304 | tf_op jit(solution)/shard_map/psum | solution.py:56
  101.5 40.8 %psum.30 = f32[16,768]{1,0:T(8,128)S(1)} all-reduce(f32[16,768]{1,0:T(8,128)S(1)} %get-tuple-element.176), channel_id=1, replica_groups=mesh['aux'=8,'pair'=4] {'aux','pair'}, use_global_device_ids=true, to_apply=%region_8.9 | all-reduce | flops 12288 | bytes 98304 | tf_op jit(solution)/shard_map/psum | solution.py:56
  142.3 0.2 conditional.11
  142.5 43.4 %psum.31 = f32[16,768]{1,0:T(8,128)S(1)} all-reduce(f32[16,768]{1,0:T(8,128)S(1)} %get-tuple-element.177), channel_id=1, replica_groups=mesh['aux'=8,'pair'=4] {'aux','pair'}, use_global_device_ids=true, to_apply=%region_11.12 | all-reduce | flops 12288 | bytes 98304 | tf_op jit(solution)/shard_map/psum | solution.py:56
  185.9 1.3 conditional.12
  186.0 0.6 broadcast_in_dim.17
  186.6 0.7 broadcast.57
  187.2 1.4 slice.19
  188.7 0.0 all-gather.7.cloned.1.call-update
  188.7 0.0 all-gather.9.cloned.1.call-start
  188.7 57.5 %all-gather.7.cloned.1.call-done = f32[512,768]{1,0:T(8,128)} async-done(((f32[16,768]{1,0:T(8,128)}), f32[512,768]{1,0:T(8,128)}) %all-gather.7.cloned.1.call-update) | async-done | bytes 1572880 | tf_op jit(solution)/shard_map/all_gather | solution.py:63
  246.2 1.4 slice.20
  247.7 0.0 all-gather.9.cloned.1.call-update
  247.7 0.0 all-gather.11.cloned.1.call-start
  247.7 59.9 %all-gather.9.cloned.1.call-done = f32[512,768]{1,0:T(8,128)} async-done(((f32[16,768]{1,0:T(8,128)}), f32[512,768]{1,0:T(8,128)}) %all-gather.9.cloned.1.call-update) | async-done | bytes 1572880 | tf_op jit(solution)/shard_map/all_gather | solution.py:63
  307.7 1.4 slice.21
  309.1 0.0 all-gather.11.cloned.1.call-update
  309.1 0.0 reduce-scatter.2.cloned.1.call-start
  309.2 59.9 %all-gather.11.cloned.1.call-done = f32[512,768]{1,0:T(8,128)} async-done(((f32[16,768]{1,0:T(8,128)}), f32[512,768]{1,0:T(8,128)}) %all-gather.11.cloned.1.call-update) | async-done | bytes 1572880 | tf_op jit(solution)/shard_map/all_gather | solution.py:63
  369.0 3.2 conditional.15
  369.0 1.5 reduce_sum.27
  370.5 1.7 fusion.13
  372.2 9.1 %fusion.16 = f32[16,8192]{1,0:T(8,128)} fusion(bf16[384,8192]{1,0:T(8,128)(2,1)} %param.21, bf16[48,8,64,128]{3,2,1,0:T(8,128)(2,1)} %bitcast.38, f32[16,384]{1,0:T(8,128)} %get-tuple-element.180), kind=kOutput, calls=%fused_computation.24 | convolution fusion | flops 103815168 | bytes 13131776 | tf_op jit(solution)/shard_map/dot_general | solution.py:93
  381.4 0.0 reduce-scatter.2.cloned.1.call-update
  381.4 32.3 %reduce-scatter.2.cloned.1.call-done = f32[16,1024]{1,0:T(8,128)} async-done(((f32[16,8192]{1,0:T(8,128)}), f32[16,1024]{1,0:T(8,128)}) %reduce-scatter.2.cloned.1.call-update) | async-done | bytes 65552 | tf_op jit(solution)/shard_map/reduce_scatter | solution.py:94
  (12 shorter events, 0.1 us)
Async XLA Ops:
  6.5 6.0 %copy-start = (bf16[16,8192]{1,0:T(8,128)(2,1)S(1)}, bf16[16,8192]{1,0:T(8,128)(2,1)}, u32[]{:S(2)}) copy-start(bf16[16,8192]{1,0:T(8,128)(2,1)} %param.22) | copy-start | bytes 786436
  6.5 239.7 %all-gather.7.cloned.1.call-start = ((), (), s32[]{:S(2)}) async-start(), calls=%async_computation.2 | async-start | bytes 1622016 | tf_op jit(solution)/shard_map/all_gather | solution.py:63
  8.7 3.9 copy-start.3
  12.5 4.0 copy-start.2
  12.5 4.0 copy-start.1
  188.7 119.0 %all-gather.9.cloned.1.call-start = ((), (), s32[]{:S(2)}) async-start(), calls=%async_computation.3 | async-start | bytes 1622016 | tf_op jit(solution)/shard_map/all_gather | solution.py:63
  247.7 121.3 %all-gather.11.cloned.1.call-start = ((), (), s32[]{:S(2)}) async-start(), calls=%async_computation.4 | async-start | bytes 1622016 | tf_op jit(solution)/shard_map/all_gather | solution.py:63
  309.1 104.6 %reduce-scatter.2.cloned.1.call-start = ((), (), s32[]{:S(2)}) async-start(), calls=%async_computation.1 | async-start | bytes 589824 | tf_op jit(solution)/shard_map/reduce_scatter | solution.py:94
Sparse Core Ops, SparseCore 0:
  188.8 57.3 all-gather.6
  249.1 58.4 all-gather.8
  310.5 58.4 all-gather.10
  381.5 32.1 reduce-scatter.1

commit v2 on v0

--- a/solution.py
+++ b/solution.py
@@ -2,6 +2,7 @@
 import jax.numpy as jnp
 from jax import lax
 from jax.sharding import PartitionSpec as P
+from jax.lax import psum
 
 TILE = 128
 SOLVE_BLOCKS = 4
@@ -53,7 +54,10 @@
             return zero_block
 
         summand = lax.cond(my_block == k, on_group, off_group, solved)
-        arrived = lax.psum(summand, ("aux", "pair"))
+        _enter_pieces_all = lambda x_in, link_axis, device_axis: psum(
+            psum(x_in, link_axis), device_axis
+        )
+        arrived = _enter_pieces_all(summand, "pair", "aux")
         solved = lax.dynamic_update_slice_in_dim(solved, arrived, k * block_size, 1)
     own_coef = jnp.zeros((count, height), jnp.float32)
     contrib = jnp.zeros((count, total), jnp.float32)

time: 372 us -> 365 us (0.981)
  blocking collectives: 297 us -> 289 us
    psum x4 -> x8, blocking collectives: 167 us -> 162 us  [the longest x4 91 us: shards(): psum(psum(x_in, link_axis), device_axis)]
where the time goes in v2:
time: 365 us; the launch traced here: 364 us
  blocking collectives  289 us (79%)
  waiting for transfers between devices  34.2 us (9%)
  matrix products  16.6 us (5%)
  between operations  13.6 us (4%)
  local copies, waits for them, and re-layouts  7.62 us (2%)
    psum x3, blocking collectives, shards(): behind = lax.psum(portion, ('aux', 'pair'))  127 us
    psum x4, blocking collectives, shards(): psum(psum(x_in, link_axis), device_axis)  91 us
    psum x4, blocking collectives, shards(): psum(x_in, link_axis)  71.4 us
    reduce_scatter x1, waiting for transfers between devices, shards(): result = lax.psum_scatter(summand, 'aux', scatter_dimension=1, tiled=True)  34.1 us
    dot_general x1, matrix products, shards(): summand = jnp.dot(rounded, masked, preferred_element_type=jnp.float32)  9.11 us
  transfers between devices with their start and end apart: 1, of which 1 were waited for; matrix products, arithmetic and copies ran while one was open for 0% of the time, Pallas kernels for 0%

profile of v2, /device:TPU:0, one launch (start us, length us, event | category | flops | bytes accessed | tf_op | source)
XLA Modules:
  0.0 363.7 jit_solution(6197303659257777566)
XLA Ops:
  6.5 0.0 copy-start
  6.5 0.0 reduce-scatter.2.cloned.1.call-start
  6.6 0.7 convert_element_type.40
  7.3 1.3 broadcast_select_fusion
  8.7 0.0 copy-start.3
  8.7 3.8 %broadcast_in_dim.25 = bf16[384,64,128]{2,1,0:T(8,128)(2,1)S(1)} broadcast(bf16[384,64]{1,0:T(8,128)(2,1)S(1)} %bitcast.36), dimensions={0,1} | broadcast | bytes 6340608 | tf_op jit(solution)/shard_map/broadcast_in_dim | solution.py:23
  12.5 0.0 copy-start.2
  12.5 0.0 copy-done
  12.5 0.0 copy-done.3
  12.5 0.0 copy-start.1
  12.6 4.0 %fusion.18 = f32[16,384]{1,0:T(8,128)S(1)} fusion(bf16[16,8192]{1,0:T(8,128)(2,1)S(1)} %copy-done, bf16[384,8192]{1,0:T(8,128)(2,1)S(1)} %copy-done.3, bf16[48,8,64,128]{3,2,1,0:T(8,128)(2,1)S(1)} %bitcast.34), kind=kOutput, calls=%fused_computation.26 | convolution fusion | flops 103809024 | bytes 12869632 | tf_op jit(solution)/shard_map/dot_general | solution.py:25
  16.5 0.0 copy-done.2
  16.5 0.0 copy-done.1
  16.5 1.8 conditional.8
  16.6 1.1 convolution_subtract_fusion
  17.6 0.7 fusion.22
  18.3 21.3 %psum.77 = f32[16,768]{1,0:T(8,128)S(1)} all-reduce(f32[16,768]{1,0:T(8,128)S(1)} %get-tuple-element.168), channel_id=1, replica_groups=mesh['aux'=8,'pair'=4] {'pair'}, use_global_device_ids=true, to_apply=%region_2.3 | all-reduce | flops 12288 | bytes 98304 | tf_op jit(solution)/shard_map/psum | solution.py:58
  39.6 22.8 %psum.78 = f32[16,768]{1,0:T(8,128)S(1)} all-reduce(f32[16,768]{1,0:T(8,128)S(1)} %psum.77), channel_id=1, replica_groups=mesh['aux'=8,'pair'=4] {'aux'}, use_global_device_ids=true, to_apply=%region_3.4 | all-reduce | flops 12288 | bytes 98304 | tf_op jit(solution)/shard_map/psum | solution.py:57
  62.4 16.1 %psum.79 = f32[16,768]{1,0:T(8,128)S(1)} all-reduce(f32[16,768]{1,0:T(8,128)S(1)} %get-tuple-element.169), channel_id=1, replica_groups=mesh['aux'=8,'pair'=4] {'pair'}, use_global_device_ids=true, to_apply=%region_6.7 | all-reduce | flops 12288 | bytes 98304 | tf_op jit(solution)/shard_map/psum | solution.py:58
  78.6 22.8 %psum.80 = f32[16,768]{1,0:T(8,128)S(1)} all-reduce(f32[16,768]{1,0:T(8,128)S(1)} %psum.79), channel_id=1, replica_groups=mesh['aux'=8,'pair'=4] {'aux'}, use_global_device_ids=true, to_apply=%region_7.8 | all-reduce | flops 12288 | bytes 98304 | tf_op jit(solution)/shard_map/psum | solution.py:57
  101.4 17.9 %psum.81 = f32[16,768]{1,0:T(8,128)S(1)} all-reduce(f32[16,768]{1,0:T(8,128)S(1)} %get-tuple-element.170), channel_id=1, replica_groups=mesh['aux'=8,'pair'=4] {'pair'}, use_global_device_ids=true, to_apply=%region_10.11 | all-reduce | flops 12288 | bytes 98304 | tf_op jit(solution)/shard_map/psum | solution.py:58
  119.3 22.7 %psum.82 = f32[16,768]{1,0:T(8,128)S(1)} all-reduce(f32[16,768]{1,0:T(8,128)S(1)} %psum.81), channel_id=1, replica_groups=mesh['aux'=8,'pair'=4] {'aux'}, use_global_device_ids=true, to_apply=%region_11.12 | all-reduce | flops 12288 | bytes 98304 | tf_op jit(solution)/shard_map/psum | solution.py:57
  142.0 0.2 conditional.11
  142.3 16.1 %psum.83 = f32[16,768]{1,0:T(8,128)S(1)} all-reduce(f32[16,768]{1,0:T(8,128)S(1)} %get-tuple-element.171), channel_id=1, replica_groups=mesh['aux'=8,'pair'=4] {'pair'}, use_global_device_ids=true, to_apply=%region_14.15 | all-reduce | flops 12288 | bytes 98304 | tf_op jit(solution)/shard_map/psum | solution.py:58
  158.4 22.7 %psum.84 = f32[16,768]{1,0:T(8,128)S(1)} all-reduce(f32[16,768]{1,0:T(8,128)S(1)} %psum.83), channel_id=1, replica_groups=mesh['aux'=8,'pair'=4] {'aux'}, use_global_device_ids=true, to_apply=%region_15.16 | all-reduce | flops 12288 | bytes 98304 | tf_op jit(solution)/shard_map/psum | solution.py:57
  181.1 1.3 conditional.12
  181.1 0.6 broadcast_in_dim.17
  181.7 0.7 broadcast.57
  182.4 0.8 slice.19
  183.2 39.5 %psum.85 = f32[16,768]{1,0:T(8,128)S(1)} all-reduce(f32[16,768]{1,0:T(8,128)S(1)} %slice.19), channel_id=1, replica_groups=mesh['aux'=8,'pair'=4] {'aux','pair'}, use_global_device_ids=true, to_apply=%region_18.19 | all-reduce | flops 12288 | bytes 98304 | tf_op jit(solution)/shard_map/psum | solution.py:67
  222.8 0.8 slice.20
  223.6 44.8 %psum.86 = f32[16,768]{1,0:T(8,128)S(1)} all-reduce(f32[16,768]{1,0:T(8,128)S(1)} %slice.20), channel_id=1, replica_groups=mesh['aux'=8,'pair'=4] {'aux','pair'}, use_global_device_ids=true, to_apply=%region_21.22 | all-reduce | flops 12288 | bytes 98304 | tf_op jit(solution)/shard_map/psum | solution.py:67
  268.4 0.8 slice.21
  269.2 42.7 %psum.87 = f32[16,768]{1,0:T(8,128)S(1)} all-reduce(f32[16,768]{1,0:T(8,128)S(1)} %slice.21), channel_id=1, replica_groups=mesh['aux'=8,'pair'=4] {'aux','pair'}, use_global_device_ids=true, to_apply=%region_24.25 | all-reduce | flops 12288 | bytes 98304 | tf_op jit(solution)/shard_map/psum | solution.py:67
  311.9 1.7 conditional.15
  311.9 1.7 fusion.13
  313.6 9.1 %fusion.16 = f32[16,8192]{1,0:T(8,128)} fusion(bf16[384,8192]{1,0:T(8,128)(2,1)} %param.21, bf16[48,8,64,128]{3,2,1,0:T(8,128)(2,1)} %bitcast.35, f32[16,384]{1,0:T(8,128)} %get-tuple-element.174), kind=kOutput, calls=%fused_computation.24 | convolution fusion | flops 103815168 | bytes 13131776 | tf_op jit(solution)/shard_map/dot_general | solution.py:96
  322.7 0.0 reduce-scatter.2.cloned.1.call-update
  322.7 34.1 %reduce-scatter.2.cloned.1.call-done = f32[16,1024]{1,0:T(8,128)} async-done(((f32[16,8192]{1,0:T(8,128)}), f32[16,1024]{1,0:T(8,128)}) %reduce-scatter.2.cloned.1.call-update) | async-done | bytes 65552 | tf_op jit(solution)/shard_map/reduce_scatter | solution.py:97
  (12 shorter events, 0.1 us)
Async XLA Ops:
  6.5 6.0 %copy-start = (bf16[16,8192]{1,0:T(8,128)(2,1)S(1)}, bf16[16,8192]{1,0:T(8,128)(2,1)}, u32[]{:S(2)}) copy-start(bf16[16,8192]{1,0:T(8,128)(2,1)} %param.22) | copy-start | bytes 786436
  6.5 350.4 %reduce-scatter.2.cloned.1.call-start = ((), (), s32[]{:S(2)}) async-start(), calls=%async_computation.1 | async-start | bytes 589824 | tf_op jit(solution)/shard_map/reduce_scatter | solution.py:97
  8.7 3.9 %copy-start.3 = (bf16[384,8192]{1,0:T(8,128)(2,1)S(1)}, bf16[384,8192]{1,0:T(8,128)(2,1)}, u32[]{:S(2)}) copy-start(bf16[384,8192]{1,0:T(8,128)(2,1)} %param.21) | copy-start | bytes 18874372
  12.5 4.0 %copy-start.2 = (bf16[384,64,128]{2,1,0:T(8,128)(2,1)}, bf16[384,64,128]{2,1,0:T(8,128)(2,1)S(1)}, u32[]{:S(2)}) copy-start(bf16[384,64,128]{2,1,0:T(8,128)(2,1)S(1)} %broadcast_in_dim.25) | copy-start | bytes 18874372
  12.5 4.0 %copy-start.1 = (f32[384,768]{1,0:T(8,128)S(1)}, f32[384,768]{1,0:T(8,128)}, u32[]{:S(2)}) copy-start(f32[384,768]{1,0:T(8,128)} %param.25) | copy-start | bytes 3538948
Sparse Core Ops, SparseCore 0:
  322.9 33.9 reduce-scatter.1
